TPU v7x, 32 devices: a whole 2x2x4 slice. The times are simulated.
32 devices in a mesh: tm: 16 (over z, y, core), series: 2 (over x).
Axes of the slice: x: 2, y: 2, z: 4, core: 2. Of those that a mesh axis runs over, the one named last changes fastest.
Arguments:
- history: bfloat16 [4, 4096, 1024], P('series', 'tm'), may hold values from -36 to 36
- lengths: int32 [4], P('series'), may hold values from 512 to 4096
- head_window: int32 [16], replicated, may hold values from 32 to 512, as said below
- input_proj: bfloat16 [1024, 3072], replicated
- output_proj: bfloat16 [1024, 1024], replicated, may hold values from -0.1875 to 0.1875
- mixer_down: bfloat16 [1024, 512], replicated, may hold values from -0.1875 to 0.1875
- mixer_up: bfloat16 [512, 1024], replicated, may hold values from -0.25 to 0.25
- series_mix: bfloat16 [4, 4], replicated, may hold values from -3 to 3
Outputs:
- layer_out: bfloat16 [4, 4096, 1024], P('series', 'tm')
Inputs may be any that keep to these rules, and one draw needn't show every extreme that they name: `head_window`: some head has exactly 512.
All inputs are finite; a program needn't handle non-finite values.
Results may differ from a plain program's by a relative error of at most 0.0065.
Values may be sent and summed in bfloat16 or wider, within the bound.
No kernel may reach another device: no remote copies, remote signals or barrier semaphores. Data moves between devices by JAX's collectives and lax.ppermute only.
A program may use at most 128 MiB of HBM per device.

v0:
```python
import functools
import math

import jax
import jax.numpy as jnp
from jax import lax
from jax.experimental import pallas as pl
from jax.experimental.pallas import tpu as pltpu
from jax.sharding import PartitionSpec as P

HEADS = 16
WINDOW = 512
LANES = 128
MASKED = -1e30


def routes(count):
    place = lambda quad, chip, core: 4 * quad + 2 * chip + core
    last = count // 4 - 1
    chip_swap = [(i, i ^ 2) for i in range(count)]
    core_swap = [(i, i ^ 1) for i in range(count)]
    near, far, far_cross = [], [], []
    for i in range(count):
        quad, chip, core = i // 4, (i // 2) % 2, i % 2
        down = quad - 1 if quad > 0 else None
        up = quad + 1 if quad < last else None
        near_quad, far_quad = (down, up) if chip == 0 else (up, down)
        if near_quad is not None:
            near.append((i, place(near_quad, chip, core)))
        if far_quad is not None:
            far.append((i, place(far_quad, chip, core)))
            if core != chip:
                far_cross.append((i, place(far_quad, chip, chip)))
    return chip_swap, core_swap, near, far, far_cross


def project(first, beside, weight, scale):
    rows, width = first.shape
    chunk = min(256, width)
    steps = width // chunk

    def body(first_ref, beside_ref, wq_ref, wk_ref, wv_ref, q_ref, k_ref, v_ref):
        def dot(block, ref):
            return jnp.dot(block[...], ref[...], preferred_element_type=jnp.float32)

        q_ref[...] = (dot(first_ref, wq_ref) * scale).astype(jnp.bfloat16)
        for index, block in enumerate((first_ref, beside_ref)):
            k_ref[index] = dot(block, wk_ref).astype(jnp.bfloat16)
            v_ref[index] = dot(block, wv_ref).astype(jnp.bfloat16).T

    whole = pl.BlockSpec((rows, width), lambda g: (0, 0))
    weights = [
        pl.BlockSpec((width, chunk), lambda g, part=part: (0, part * steps + g))
        for part in range(3)
    ]
    return pl.pallas_call(
        body,
        out_shape=(
            jax.ShapeDtypeStruct((rows, width), jnp.bfloat16),
            jax.ShapeDtypeStruct((2, rows, width), jnp.bfloat16),
            jax.ShapeDtypeStruct((2, width, rows), jnp.bfloat16),
        ),
        grid=(steps,),
        in_specs=[whole, whole] + weights,
        out_specs=(
            pl.BlockSpec((rows, chunk), lambda g: (0, g)),
            pl.BlockSpec((2, rows, chunk), lambda g: (0, 0, g)),
            pl.BlockSpec((2, chunk, rows), lambda g: (0, g, 0)),
        ),
        cost_estimate=pl.CostEstimate(
            flops=10 * rows * width * width, bytes_accessed=6 * width * width, transcendentals=0
        ),
        name="project",
    )(first, beside, weight, weight, weight)


def attend(
    place, head_window, lengths, weight, output_proj, mixer_down, scale, home, raw, ready,
    own=None, keep=0,
):
    raw_sides = [side for side, _ in raw]
    ready_sides = [side for side, _ in ready]
    raw = [block for _, blocks in raw for block in blocks]
    ready = [arrays for _, arrays in ready]
    rows, width = raw[0].shape
    devices = lax.axis_size("tm")
    head_size = width // HEADS
    chunk = 2 * LANES
    chunks = width // chunk
    pairs = chunk // LANES
    reach = WINDOW // rows
    steps = 2 * reach + 1
    slot_count = steps + 1
    half_rows = rows // 2
    cols = 2 * half_rows
    raw_count, ready_count = len(raw), len(ready)

    def span(step, half):
        if step == 0 and half == 1:
            return half_rows, rows
        if step == steps - 1 and half == 0:
            return 0, half_rows
        return 0, rows

    def body(place_ref, window_ref, length_ref, *refs):
        refs = list(refs)
        take = lambda count: [refs.pop(0) for _ in range(count)]
        raw_refs = take(raw_count)
        ready_refs = take(2 * ready_count)
        rows_ref, query_ref = take(2) if home else (raw_refs[0], None)
        wq_ref = None if home else take(1)[0]
        wk_ref, wv_ref, wo_hbm, down_hbm = take(4)
        hidden_ref, branch_ref = take(2)
        keep_refs = take(2) if keep else None
        key_scr, row_scr, query_scr = take(3)
        value_scrs, score_scrs, top_scrs = take(2), take(2), take(2)
        attended_scr, update_scr, wo_scr, down_scr, copy_sems = take(5)
        index = pl.program_id(0)
        position = place_ref[0]
        core = position % 2
        chip = (position // 2) % 2
        patches = rows * devices
        valid_first = patches - length_ref[chip]
        query_chip = chip if home else 1 - chip
        query_first = (position - 2 * chip + 2 * query_chip) * rows

        def slot_of(side, beside):
            offset = core if not beside else 1 - core
            return 2 + 2 * side * (1 - 2 * chip) + offset

        copies = [
            pltpu.make_async_copy(wo_hbm, wo_scr, copy_sems.at[0]),
            pltpu.make_async_copy(down_hbm, down_scr, copy_sems.at[1]),
        ]

        @pl.when(index == 0)
        def _():
            for copy in copies:
                copy.start()
            row_scr[...] = lax.broadcasted_iota(jnp.int32, (rows, LANES), 0)

        def front(value_scr, score_scr, top_scr):
            units = []
            state = {}

            def ready_blocks():
                for number in range(ready_count):
                    for which in range(2):
                        slot = slot_of(ready_sides[number], which)
                        key_scr[slot] = ready_refs[2 * number][which]
                        value_scr[slot] = ready_refs[2 * number + 1][which]

            units.append(ready_blocks)

            def project_queries():
                both = jnp.dot(raw_refs[0][...], wq_ref[...], preferred_element_type=jnp.float32)
                query_scr[...] = (both * scale).astype(jnp.bfloat16)

            if query_ref is None:
                units.append(project_queries)

            def project_keys(number):
                slot = slot_of(raw_sides[number // 2], number % 2)
                keys = jnp.dot(
                    raw_refs[number][...], wk_ref[...], preferred_element_type=jnp.float32
                ).astype(jnp.bfloat16)
                key_scr[slot] = keys
                if number < keep:
                    keep_refs[0][number] = keys

            def project_values(number):
                slot = slot_of(raw_sides[number // 2], number % 2)
                values = jnp.dot(
                    raw_refs[number][...], wv_ref[...], preferred_element_type=jnp.float32
                ).astype(jnp.bfloat16).T
                value_scr[slot] = values
                if number < keep:
                    keep_refs[1][number] = values

            for project in (project_keys, project_values):
                for number in range(raw_count):
                    units.append(functools.partial(project, number))
            early = len(units)

            def bounds(pair, half):
                column = lax.broadcasted_iota(jnp.int32, (1, cols), 1)
                second = column >= half_rows
                head = 2 * (pairs * index + pair)
                window = jnp.where(second, window_ref[head + 1], window_ref[head])
                lane = lax.broadcasted_iota(jnp.int32, (half_rows, LANES), 1)
                local = jnp.where(second, column - half_rows, column) + half * half_rows
                lowest = jnp.maximum(local - window, valid_first - query_first)
                highest = jnp.minimum(local + window, patches - 1 - query_first)
                where = slice(half * half_rows, (half + 1) * half_rows)
                source = query_scr if query_ref is None else query_ref
                part = source[where, pair * LANES : (pair + 1) * LANES]
                zero = jnp.zeros_like(part)
                right = jnp.concatenate(
                    [
                        jnp.where(lane < head_size, part, zero),
                        jnp.where(lane < head_size, zero, part),
                    ],
                    0,
                )
                return right, lowest, highest

            def score_block(pair, half, step):
                if step == 0:
                    state["bounds"] = bounds(pair, half)
                right, lowest, highest = state["bounds"]
                start, stop = span(step, half)
                first = (step - reach) * rows
                scores = lax.dot_general(
                    key_scr[core + step, start:stop, pair * LANES : (pair + 1) * LANES],
                    right,
                    (((1,), (1,)), ((), ())),
                    preferred_element_type=jnp.float32,
                )
                key_row = row_scr[start:stop, :]
                key_row = jnp.concatenate([key_row] * (cols // LANES), 1)
                allowed = None
                if step <= reach:
                    allowed = key_row >= lowest - first
                if step >= reach:
                    upper = key_row <= highest - first
                    allowed = upper if allowed is None else allowed & upper
                scores = jnp.where(allowed, scores, MASKED)
                score_scr[pair, half, step, start:stop, :] = scores
                top = jnp.max(scores, axis=0, keepdims=True)
                if step > 0:
                    top = jnp.maximum(state["top"], top)
                state["top"] = top
                if step == steps - 1:
                    top_scr[pair, half] = top

            for pair in range(pairs):
                for half in range(2):
                    for step in range(steps):
                        units.append(functools.partial(score_block, pair, half, step))
            return units[:early], units[early:]

        def back(value_scr, score_scr, top_scr, last=False):
            sums = [None] * (2 * pairs)

            def add_block(pair, step, head):
                where = slice(head * half_rows, (head + 1) * half_rows)
                parts = []
                for half in range(2):
                    start, stop = span(step, half)
                    part = jnp.exp2(
                        score_scr[pair, half, step, start:stop, where]
                        - top_scr[pair, half][:, where]
                    )
                    part = [part.astype(jnp.bfloat16)]
                    if start > 0:
                        part = [jnp.zeros((start, half_rows), jnp.bfloat16)] + part
                    if stop < rows:
                        part = part + [jnp.zeros((rows - stop, half_rows), jnp.bfloat16)]
                    parts.append(jnp.concatenate(part, 0) if len(part) > 1 else part[0])
                weights = jnp.concatenate(parts, 1)
                first = pair * LANES + head * head_size
                left = jnp.concatenate(
                    [
                        value_scr[core + step, first : first + head_size, :],
                        jnp.ones((16, rows), jnp.bfloat16),
                    ],
                    0,
                )
                add = jnp.dot(left, weights, preferred_element_type=jnp.float32)
                place = 2 * pair + head
                sums[place] = add if sums[place] is None else sums[place] + add

            def write(pair):
                query_valid = (
                    lax.broadcasted_iota(jnp.int32, (1, rows), 1) >= valid_first - query_first
                )
                outs = []
                for head in range(2):
                    result = sums[2 * pair + head]
                    total = result[head_size : head_size + 1]
                    factor = jnp.where(query_valid, 1.0 / total, 0.0)
                    outs.append(result[:head_size] * factor)
                if last:
                    where = slice(width - chunk + pair * LANES, width - chunk + (pair + 1) * LANES)
                else:
                    first = (index - 1) * chunk + pair * LANES
                    where = pl.ds(pl.multiple_of(first, LANES), LANES)
                attended_scr[:, where] = jnp.concatenate(outs, 0).T.astype(jnp.bfloat16)

            units = []
            for pair in range(pairs):
                for head in range(2):
                    for step in range(steps):
                        units.append(functools.partial(add_block, pair, step, head))
                units.append(functools.partial(write, pair))
            return units

        def interleave(first, second):
            done = 0
            for number, unit in enumerate(first):
                unit()
                target = (number + 1) * len(second) // len(first)
                for other in second[done:target]:
                    other()
                done = target

        sets = [(value_scrs[n], score_scrs[n], top_scrs[n]) for n in range(2)]

        @pl.when(index == 0)
        def _():
            early, late = front(*sets[0])
            interleave(early + late, [])

        for parity in range(2):

            @pl.when((index > 0) & (index < chunks) & (index % 2 == parity))
            def _():
                early, late = front(*sets[parity])
                interleave(early, back(*sets[1 - parity]))
                interleave(late, [])

        @pl.when(index == chunks)
        def _():
            for copy in copies:
                copy.wait()
            before = width - chunk

            def update_block(column):
                where = slice(column * chunk, (column + 1) * chunk)
                update_scr[:, where] = jnp.dot(
                    attended_scr[:, :before],
                    wo_scr[:before, where],
                    preferred_element_type=jnp.float32,
                )

            updates = [functools.partial(update_block, column) for column in range(chunks)]
            interleave(updates, back(*sets[(chunks - 1) % 2], last=True))
            update = update_scr[...] + jnp.dot(
                attended_scr[:, before:], wo_scr[before:, :], preferred_element_type=jnp.float32
            )
            hidden = (rows_ref[...].astype(jnp.float32) + update).astype(jnp.bfloat16)
            hidden_ref[...] = hidden
            branch_ref[...] = jnp.dot(
                hidden, down_scr[...], preferred_element_type=jnp.float32
            ).astype(jnp.bfloat16)

    ahead = lambda g: jnp.minimum(g, chunks - 1)
    block = pl.BlockSpec((rows, chunk), lambda g, *_: (0, ahead(g)))
    key_spec = lambda count: pl.BlockSpec((count, rows, chunk), lambda g, *_: (0, 0, ahead(g)))
    value_spec = lambda count: pl.BlockSpec((count, chunk, rows), lambda g, *_: (0, ahead(g), 0))
    weight_spec = lambda part: pl.BlockSpec(
        (width, chunk), lambda g, *_: (0, part * chunks + ahead(g))
    )
    in_specs = [pl.BlockSpec((rows, width), lambda g, *_: (0, 0)) for _ in raw]
    operands = list(raw)
    for keys, values in ready:
        in_specs += [key_spec(2), value_spec(2)]
        operands += [keys, values]
    whole = lambda shape: pl.BlockSpec(shape, lambda g, *_: (0, 0))
    if home:
        in_specs += [whole((rows, width)), block]
        operands += own
    else:
        in_specs.append(weight_spec(0))
        operands.append(weight)
    in_specs += [weight_spec(1), weight_spec(2)] + [pl.BlockSpec(memory_space=pl.ANY)] * 2
    operands += [weight, weight, output_proj, mixer_down]
    inner = mixer_down.shape[1]
    out_shape = [
        jax.ShapeDtypeStruct((rows, width), jnp.bfloat16),
        jax.ShapeDtypeStruct((rows, inner), jnp.bfloat16),
    ]
    out_specs = [whole((rows, width)), whole((rows, inner))]
    if keep:
        out_shape += [
            jax.ShapeDtypeStruct((keep, rows, width), jnp.bfloat16),
            jax.ShapeDtypeStruct((keep, width, rows), jnp.bfloat16),
        ]
        out_specs += [key_spec(keep), value_spec(keep)]
    twice = lambda shape, dtype: [pltpu.VMEM(shape, dtype)] * 2
    return pl.pallas_call(
        body,
        out_shape=tuple(out_shape),
        grid_spec=pltpu.PrefetchScalarGridSpec(
            num_scalar_prefetch=3,
            grid=(chunks + 1,),
            in_specs=in_specs,
            out_specs=tuple(out_specs),
            scratch_shapes=[
                pltpu.VMEM((slot_count, rows, chunk), jnp.bfloat16),
                pltpu.VMEM((rows, LANES), jnp.int32),
                pltpu.VMEM((rows, chunk), jnp.bfloat16),
            ]
            + twice((slot_count, chunk, rows), jnp.bfloat16)
            + twice((pairs, 2, steps, rows, cols), jnp.float32)
            + twice((pairs, 2, 1, cols), jnp.float32)
            + [
                pltpu.VMEM((rows, width), jnp.bfloat16),
                pltpu.VMEM((rows, width), jnp.float32),
                pltpu.VMEM(output_proj.shape, jnp.bfloat16),
                pltpu.VMEM(mixer_down.shape, jnp.bfloat16),
                pltpu.SemaphoreType.DMA((2,)),
            ],
        ),
        cost_estimate=pl.CostEstimate(
            flops=(8 * steps * rows + 4 * raw_count * width) * rows * width,
            bytes_accessed=4 * width * width + 4 * steps * rows * width,
            transcendentals=steps * rows * rows * HEADS,
        ),
        name="attend",
    )(place, head_window, lengths, *operands)


def on_device(
    history, lengths, head_window, input_proj, output_proj, mixer_down, mixer_up, series_mix
):
    local_series, rows, width = history.shape
    devices = lax.axis_size("tm")
    groups = lax.axis_size("series")
    assert local_series == 2 and devices % 4 == 0 and WINDOW == 2 * rows
    position = lax.axis_index("tm")
    chip = (position // 2) % 2
    chip_swap, core_swap, near_route, far_route, far_cross = routes(devices)

    def move(block, route):
        return lax.ppermute(block, "tm", route)

    def part(array, index):
        return lax.dynamic_index_in_dim(array, index, 0, keepdims=False)

    mine = part(history, chip)
    other = part(history, 1 - chip)
    away = move(other, chip_swap)
    near = move(mine, near_route)
    mine_beside = move(mine, core_swap)
    scale = (width // HEADS) ** (-0.5) * math.log2(math.e)
    place = position.astype(jnp.int32)[None]
    attention = functools.partial(
        attend, place, head_window, lengths, input_proj, output_proj, mixer_down, scale
    )

    home_queries, *home_ready = project(mine, mine_beside, input_proj, scale)
    away, home_queries = lax.optimization_barrier((away, home_queries))
    away_beside = move(away, core_swap)
    near, away_beside = lax.optimization_barrier((near, away_beside))
    near_beside = move(near, core_swap)
    far = move(away, far_route)
    far_beside = move(away, far_cross)
    away_hidden, away_branch, *away_ready = attention(
        False,
        [(0, [away, away_beside]), (1, [near, near_beside])],
        [(-1, home_ready)],
        keep=2,
    )
    away_hidden, far, far_beside = lax.optimization_barrier((away_hidden, far, far_beside))

    def down(hidden):
        return jnp.dot(hidden, mixer_down, preferred_element_type=jnp.float32).astype(jnp.bfloat16)

    other_hidden = move(away_hidden, chip_swap)
    other_branches = []
    for shift in range(1, groups):
        route = [
            (i * groups + (g + shift) % groups, home * groups + g)
            for g in range(groups)
            for i, home in chip_swap
        ]
        other_branches.append(lax.ppermute(away_branch, ("tm", "series"), route))

    mine_hidden, mine_branch = attention(
        True,
        [(-1, [far, far_beside])],
        [(0, home_ready), (1, away_ready)],
        own=[mine, home_queries],
    )
    mine_branches = [mine_branch]
    for shift in range(1, groups):
        route = [((g + shift) % groups, g) for g in range(groups)]
        mine_branches.append(lax.ppermute(mine_branch, "series", route))
    other_hidden, mine_branch = lax.optimization_barrier((other_hidden, mine_branch))
    other_branches = [down(other_hidden)] + other_branches

    own_group = lax.axis_index("series")
    hidden = jnp.where(
        chip == 0,
        jnp.stack([mine_hidden, other_hidden]),
        jnp.stack([other_hidden, mine_hidden]),
    )
    rows_of_mix = lax.dynamic_slice_in_dim(series_mix.astype(jnp.float32), 2 * own_group, 2, 0)
    combined = 0.0
    for branches, series in ((mine_branches, chip), (other_branches, 1 - chip)):
        for shift, branch in enumerate(branches):
            group = (own_group + shift) % groups
            factor = lax.dynamic_slice_in_dim(rows_of_mix, 2 * group + series, 1, 1)
            combined += factor[:, :, None] * branch.astype(jnp.float32)[None]
    combined = lax.optimization_barrier(combined.astype(jnp.bfloat16))
    update = jnp.einsum("spc,cd->spd", combined, mixer_up, preferred_element_type=jnp.float32)
    return (hidden.astype(jnp.float32) + update).astype(jnp.bfloat16)


def solution(mesh):
    in_specs = (P("series", "tm", None), P("series"), P(), P(), P(), P(), P(), P())
    out_specs = P("series", "tm", None)
    return jax.shard_map(
        on_device, mesh=mesh, in_specs=in_specs, out_specs=out_specs, check_vma=False
    )
```

profile of v0, /device:TPU:0, one launch (start us, length us, event | category | flops | bytes accessed | tf_op | source)
XLA Modules:
  0.0 73.3 jit_solution(9218205357085122335)
XLA Ops:
  0.0 2.2 %dynamic-slice_bitcast_fusion = (bf16[256,1024]{1,0:T(8,128)(2,1)S(1)}, bf16[256,1024]{1,0:T(8,128)(2,1)}) fusion(bf16[2,256,1024]{2,1,0:T(8,128)(2,1)} %param.8, s32[]{:T(128)S(6)} %select_n.67, s32[]{:T(128)S(6)} %select_n.66), kind=kLoop, calls=%fused_computation.6 | loop fusion | bytes 2097160 | tf_op jit(solution)/shard_map/jit(dynamic_index_in_dim)/squeeze | solution.py:429
  2.2 0.5 collective-permute-start.1
  2.7 2.5 %collective-permute-start = (bf16[256,1024]{1,0:T(8,128)(2,1)}, bf16[256,1024]{1,0:T(8,128)(2,1)S(1)}, u32[]{:S(2)}, u32[]{:S(2)}) collective-permute-start(bf16[256,1024]{1,0:T(8,128)(2,1)} %get-tuple-element.44), channel_id=1, source_target_pairs={{0,4},{2,6},{4,0},{6,2},{8,12},{10,14},{12,8},{14,10},{16,20},{18,... | collective-permute-start | bytes 1572872 | tf_op jit(solution)/shard_map/ppermute | solution.py:426
  5.2 1.3 %collective-permute-start.2 = (bf16[256,1024]{1,0:T(8,128)(2,1)S(1)}, bf16[256,1024]{1,0:T(8,128)(2,1)S(1)}, u32[]{:S(2)}, u32[]{:S(2)}) collective-permute-start(bf16[256,1024]{1,0:T(8,128)(2,1)S(1)} %get-tuple-element.43.first_ref.refs_6_), channel_id=1, source_target_pairs={{4,12},{6,14},{8,0},{10,2},{12,20},{14,22},{16,8},{18,10},{20,28},... | collective-permute-start | bytes 1572872 | tf_op jit(solution)/shard_map/ppermute | solution.py:426
  6.5 0.0 collective-permute-done.1.beside_ref
  6.5 0.8 %copy-done.9 = bf16[256,1024]{1,0:T(8,128)(2,1)} copy-done((bf16[256,1024]{1,0:T(8,128)(2,1)}, bf16[256,1024]{1,0:T(8,128)(2,1)S(1)}, u32[]{:S(2)}) %copy-start.9) | copy-done | bytes 524312
  7.3 7.0 %project.1 = (bf16[256,1024]{1,0:T(8,128)(2,1)}, bf16[2,256,1024]{2,1,0:T(8,128)(2,1)}, bf16[2,1024,256]{2,1,0:T(8,128)(2,1)}) custom-call(bf16[256,1024]{1,0:T(8,128)(2,1)} %copy-done.2, bf16[256,1024]{1,0:T(8,128)(2,1)} %copy-done.9, bf16[1024,3072]{1,0:T(8,128)(2,1)} %refs_9_.3, bf16[1024,3072]{1,0:T(8,128)(2,1)} %refs_9_.3, bf16[1024,3072]{1,0:T(8,128)(2,1)} %refs_9_.3), custom_call_target="tpu_custom_call" | custom-call | flops 2684354560 | bytes 6291456 | tf_op jit(solution)/shard_map/project/pallas_call | solution.py:56
  14.3 3.7 %collective-permute-done.refs_0_ = bf16[256,1024]{1,0:T(8,128)(2,1)S(1)} collective-permute-done((bf16[256,1024]{1,0:T(8,128)(2,1)}, bf16[256,1024]{1,0:T(8,128)(2,1)S(1)}, u32[]{:S(2)}, u32[]{:S(2)}) %collective-permute-start) | collective-permute-done | bytes 524320 | tf_op jit(solution)/shard_map/ppermute | solution.py:426
  18.0 0.0 collective-permute-start.3
  18.0 3.1 %collective-permute-done.2.refs_2_ = bf16[256,1024]{1,0:T(8,128)(2,1)S(1)} collective-permute-done((bf16[256,1024]{1,0:T(8,128)(2,1)S(1)}, bf16[256,1024]{1,0:T(8,128)(2,1)S(1)}, u32[]{:S(2)}, u32[]{:S(2)}) %collective-permute-start.2) | collective-permute-done | bytes 524320 | tf_op jit(solution)/shard_map/ppermute | solution.py:426
  21.1 0.1 collective-permute-start.4
  21.2 3.5 %collective-permute-start.5 = (bf16[256,1024]{1,0:T(8,128)(2,1)S(1)}, bf16[256,1024]{1,0:T(8,128)(2,1)S(1)}, u32[]{:S(2)}, u32[]{:S(2)}) collective-permute-start(bf16[256,1024]{1,0:T(8,128)(2,1)S(1)} %collective-permute-done.refs_0_), channel_id=1, source_target_pairs={{0,8},{2,10},{8,16},{10,18},{12,4},{14,6},{16,24},{18,26},{20,12},... | collective-permute-start | bytes 1572872 | tf_op jit(solution)/shard_map/ppermute | solution.py:426
  24.7 0.7 collective-permute-start.6
  25.4 0.0 collective-permute-done.4.refs_3_
  25.5 0.8 %copy-done.8 = bf16[256,1024]{1,0:T(8,128)(2,1)} copy-done((bf16[256,1024]{1,0:T(8,128)(2,1)}, bf16[256,1024]{1,0:T(8,128)(2,1)S(1)}, u32[]{:S(2)}) %copy-start.8) | copy-done | bytes 524312
  26.3 15.8 %attend.2 = (bf16[256,1024]{1,0:T(8,128)(2,1)}, bf16[256,512]{1,0:T(8,128)(2,1)}, bf16[2,256,1024]{2,1,0:T(8,128)(2,1)}, bf16[2,1024,256]{2,1,0:T(8,128)(2,1)}) custom-call(s32[1]{0:T(128)} %bitcast.place_ref, s32[16]{0:T(128)} %window_ref.3, s32[2]{0:T(128)} %length_ref.3, bf16[256,1024]{1,0:T(8,128)(2,1)} %copy-done.3, bf16[256,1024]{1,0:T(8,128)(2,1)} %copy-done.7, ...), custom_call_target="tpu_custom_call" | custom-call | flops 6979321856 | bytes 9437184 | tf_op jit(solution)/shard_map/attend/pallas_call | solution.py:381
  42.0 0.0 collective-permute-done.5.refs_0_
  42.1 0.1 collective-permute-start.7
  42.1 0.7 copy-done.5
  42.9 0.2 copy-done.6
  43.1 13.4 %attend.3 = (bf16[256,1024]{1,0:T(8,128)(2,1)}, bf16[256,512]{1,0:T(8,128)(2,1)}) custom-call(s32[1]{0:T(128)} %bitcast.place_ref, s32[16]{0:T(128)} %window_ref.3, s32[2]{0:T(128)} %length_ref.3, bf16[256,1024]{1,0:T(8,128)(2,1)} %copy-done.5, bf16[256,1024]{1,0:T(8,128)(2,1)} %copy-done.6, bf16[2,256,1024]{2,1,0:T(8,128)(2,1)} %get-tuple-element.26.refs_4_.refs_2_, ...), custom_call_target="tpu_custom_call" | custom-call | flops 4831838208 | bytes 9437184 | tf_op jit(solution)/shard_map/attend/pallas_call | solution.py:381
  56.4 0.0 copy-start.1
  56.5 1.5 %collective-permute-start.8 = (bf16[256,512]{1,0:T(8,128)(2,1)}, bf16[256,512]{1,0:T(8,128)(2,1)S(1)}, u32[]{:S(2)}, u32[]{:S(2)}) collective-permute-start(bf16[256,512]{1,0:T(8,128)(2,1)} %get-tuple-element.36), channel_id=1, source_target_pairs={{1,0},{0,1},{3,2},{2,3},{5,4},{4,5},{7,6},{6,7},{9,8},{8,9},{11,10... | collective-permute-start | bytes 786440 | tf_op jit(solution)/shard_map/ppermute | solution.py:479
  58.0 1.2 %collective-permute-start.9 = (bf16[256,512]{1,0:T(8,128)(2,1)S(1)}, bf16[256,512]{1,0:T(8,128)(2,1)S(1)}, u32[]{:S(2)}, u32[]{:S(2)}) collective-permute-start(bf16[256,512]{1,0:T(8,128)(2,1)S(1)} %copy-done.12), channel_id=1, source_target_pairs={{1,4},{3,6},{5,0},{7,2},{9,12},{11,14},{13,8},{15,10},{17,20},{19,... | collective-permute-start | bytes 786440 | tf_op jit(solution)/shard_map/ppermute | solution.py:468
  59.1 0.2 dynamic-slice_reduce_fusion.3
  59.4 1.0 %convert_element_type.29 = f32[256,512]{1,0:T(8,128)S(1)} convert(bf16[256,512]{1,0:T(8,128)(2,1)} %get-tuple-element.36) | non-fusion elementwise | flops 131072 | bytes 786432 | tf_op jit(solution)/shard_map/convert_element_type | solution.py:495
  60.4 3.6 %collective-permute-done.8 = bf16[256,512]{1,0:T(8,128)(2,1)S(1)} collective-permute-done((bf16[256,512]{1,0:T(8,128)(2,1)}, bf16[256,512]{1,0:T(8,128)(2,1)S(1)}, u32[]{:S(2)}, u32[]{:S(2)}) %collective-permute-start.8) | collective-permute-done | bytes 262176 | tf_op jit(solution)/shard_map/ppermute | solution.py:479
  64.0 6.4 %collective-permute-done.9 = bf16[256,512]{1,0:T(8,128)(2,1)S(1)} collective-permute-done((bf16[256,512]{1,0:T(8,128)(2,1)S(1)}, bf16[256,512]{1,0:T(8,128)(2,1)S(1)}, u32[]{:S(2)}, u32[]{:S(2)}) %collective-permute-start.9) | collective-permute-done | bytes 262176 | tf_op jit(solution)/shard_map/ppermute | solution.py:468
  70.6 0.4 fusion
  71.0 0.3 add_convert_fusion.1
  71.3 0.2 copy-done.11
  71.6 1.8 %add_convert_fusion = bf16[2,256,1024]{2,1,0:T(8,128)(2,1)} fusion(bf16[2,256,512]{2,1,0:T(8,128)(2,1)S(1)} %add_convert_fusion.1, bf16[1,256,1024]{2,1,0:T(8,128)(2,1)S(1)} %bitcast.13, bf16[1,256,1024]{2,1,0:T(8,128)(2,1)S(1)} %bitcast.14, bf16[512,1024]{1,0:T(8,128)(2,1)S(1)} %copy-done, pred[]{:T(512)S(6)} %eq.9), kind=kOutput, calls=%fused_computation | convolution fusion | flops 540016640 | bytes 3670017 | tf_op jit(solution)/shard_map/spc,cd->spd/dot_general | solution.py:497
  (26 shorter events, 0.1 us)
Async XLA Ops:
  0.0 71.3 %copy-start = (bf16[512,1024]{1,0:T(8,128)(2,1)S(1)}, bf16[512,1024]{1,0:T(8,128)(2,1)}, u32[]{:S(2)}) copy-start(bf16[512,1024]{1,0:T(8,128)(2,1)} %param.14) | copy-start | bytes 3145732
  2.2 4.3 %copy-start.2 = (bf16[256,1024]{1,0:T(8,128)(2,1)}, bf16[256,1024]{1,0:T(8,128)(2,1)S(1)}, u32[]{:S(2)}) copy-start(bf16[256,1024]{1,0:T(8,128)(2,1)S(1)} %get-tuple-element.43.first_ref.refs_6_) | copy-start | bytes 1572868
  2.2 4.3 %collective-permute-start.1 = (bf16[256,1024]{1,0:T(8,128)(2,1)S(1)}, bf16[256,1024]{1,0:T(8,128)(2,1)S(1)}, u32[]{:S(2)}, u32[]{:S(2)}) collective-permute-start(bf16[256,1024]{1,0:T(8,128)(2,1)S(1)} %get-tuple-element.43.first_ref.refs_6_), channel_id=1, source_target_pairs={{0,2},{2,0},{4,6},{6,4},{8,10},{10,8},{12,14},{14,12},{16,18},{18,... | collective-permute-start | bytes 1572872 | tf_op jit(solution)/shard_map/ppermute | solution.py:426
  2.7 15.3 %collective-permute-start = (bf16[256,1024]{1,0:T(8,128)(2,1)}, bf16[256,1024]{1,0:T(8,128)(2,1)S(1)}, u32[]{:S(2)}, u32[]{:S(2)}) collective-permute-start(bf16[256,1024]{1,0:T(8,128)(2,1)} %get-tuple-element.44), channel_id=1, source_target_pairs={{0,4},{2,6},{4,0},{6,2},{8,12},{10,14},{12,8},{14,10},{16,20},{18,... | collective-permute-start | bytes 1572872 | tf_op jit(solution)/shard_map/ppermute | solution.py:426
  5.2 15.9 %collective-permute-start.2 = (bf16[256,1024]{1,0:T(8,128)(2,1)S(1)}, bf16[256,1024]{1,0:T(8,128)(2,1)S(1)}, u32[]{:S(2)}, u32[]{:S(2)}) collective-permute-start(bf16[256,1024]{1,0:T(8,128)(2,1)S(1)} %get-tuple-element.43.first_ref.refs_6_), channel_id=1, source_target_pairs={{4,12},{6,14},{8,0},{10,2},{12,20},{14,22},{16,8},{18,10},{20,28},... | collective-permute-start | bytes 1572872 | tf_op jit(solution)/shard_map/ppermute | solution.py:426
  6.5 0.8 %copy-start.9 = (bf16[256,1024]{1,0:T(8,128)(2,1)}, bf16[256,1024]{1,0:T(8,128)(2,1)S(1)}, u32[]{:S(2)}) copy-start(bf16[256,1024]{1,0:T(8,128)(2,1)S(1)} %collective-permute-done.1.beside_ref) | copy-start | bytes 1572868
  18.0 8.3 %copy-start.3 = (bf16[256,1024]{1,0:T(8,128)(2,1)}, bf16[256,1024]{1,0:T(8,128)(2,1)S(1)}, u32[]{:S(2)}) copy-start(bf16[256,1024]{1,0:T(8,128)(2,1)S(1)} %collective-permute-done.refs_0_) | copy-start | bytes 1572868
  18.0 3.1 %collective-permute-start.3 = (bf16[256,1024]{1,0:T(8,128)(2,1)S(1)}, bf16[256,1024]{1,0:T(8,128)(2,1)S(1)}, u32[]{:S(2)}, u32[]{:S(2)}) collective-permute-start(bf16[256,1024]{1,0:T(8,128)(2,1)S(1)} %collective-permute-done.refs_0_), channel_id=1, source_target_pairs={{0,2},{2,0},{4,6},{6,4},{8,10},{10,8},{12,14},{14,12},{16,18},{18,... | collective-permute-start | bytes 1572872 | tf_op jit(solution)/shard_map/ppermute | solution.py:426
  21.1 5.1 %copy-start.4 = (bf16[256,1024]{1,0:T(8,128)(2,1)}, bf16[256,1024]{1,0:T(8,128)(2,1)S(1)}, u32[]{:S(2)}) copy-start(bf16[256,1024]{1,0:T(8,128)(2,1)S(1)} %collective-permute-done.2.refs_2_) | copy-start | bytes 1572868
  21.1 4.3 %copy-start.7 = (bf16[256,1024]{1,0:T(8,128)(2,1)}, bf16[256,1024]{1,0:T(8,128)(2,1)S(1)}, u32[]{:S(2)}) copy-start(bf16[256,1024]{1,0:T(8,128)(2,1)S(1)} %collective-permute-done.3.refs_1_) | copy-start | bytes 1572868
  21.1 4.3 %collective-permute-start.4 = (bf16[256,1024]{1,0:T(8,128)(2,1)S(1)}, bf16[256,1024]{1,0:T(8,128)(2,1)S(1)}, u32[]{:S(2)}, u32[]{:S(2)}) collective-permute-start(bf16[256,1024]{1,0:T(8,128)(2,1)S(1)} %collective-permute-done.2.refs_2_), channel_id=1, source_target_pairs={{0,2},{2,0},{4,6},{6,4},{8,10},{10,8},{12,14},{14,12},{16,18},{18,... | collective-permute-start | bytes 1572872 | tf_op jit(solution)/shard_map/ppermute | solution.py:426
  21.2 20.8 %collective-permute-start.5 = (bf16[256,1024]{1,0:T(8,128)(2,1)S(1)}, bf16[256,1024]{1,0:T(8,128)(2,1)S(1)}, u32[]{:S(2)}, u32[]{:S(2)}) collective-permute-start(bf16[256,1024]{1,0:T(8,128)(2,1)S(1)} %collective-permute-done.refs_0_), channel_id=1, source_target_pairs={{0,8},{2,10},{8,16},{10,18},{12,4},{14,6},{16,24},{18,26},{20,12},... | collective-permute-start | bytes 1572872 | tf_op jit(solution)/shard_map/ppermute | solution.py:426
  24.7 17.3 %collective-permute-start.6 = (bf16[256,1024]{1,0:T(8,128)(2,1)S(1)}, bf16[256,1024]{1,0:T(8,128)(2,1)S(1)}, u32[]{:S(2)}, u32[]{:S(2)}) collective-permute-start(bf16[256,1024]{1,0:T(8,128)(2,1)S(1)} %collective-permute-done.refs_0_), channel_id=1, source_target_pairs={{2,8},{10,16},{12,6},{18,24},{20,14},{28,22},{3,9},{11,17},{13,7},... | collective-permute-start | bytes 1572872 | tf_op jit(solution)/shard_map/ppermute | solution.py:426
  25.4 0.8 %copy-start.8 = (bf16[256,1024]{1,0:T(8,128)(2,1)}, bf16[256,1024]{1,0:T(8,128)(2,1)S(1)}, u32[]{:S(2)}) copy-start(bf16[256,1024]{1,0:T(8,128)(2,1)S(1)} %collective-permute-done.4.refs_3_) | copy-start | bytes 1572868
  42.0 0.8 %copy-start.5 = (bf16[256,1024]{1,0:T(8,128)(2,1)}, bf16[256,1024]{1,0:T(8,128)(2,1)S(1)}, u32[]{:S(2)}) copy-start(bf16[256,1024]{1,0:T(8,128)(2,1)S(1)} %collective-permute-done.5.refs_0_) | copy-start | bytes 1572868
  42.1 1.0 %copy-start.6 = (bf16[256,1024]{1,0:T(8,128)(2,1)}, bf16[256,1024]{1,0:T(8,128)(2,1)S(1)}, u32[]{:S(2)}) copy-start(bf16[256,1024]{1,0:T(8,128)(2,1)S(1)} %collective-permute-done.6.refs_1_) | copy-start | bytes 1572868
  42.1 28.5 %collective-permute-start.7 = (bf16[256,1024]{1,0:T(8,128)(2,1)}, bf16[256,1024]{1,0:T(8,128)(2,1)S(1)}, u32[]{:S(2)}, u32[]{:S(2)}) collective-permute-start(bf16[256,1024]{1,0:T(8,128)(2,1)} %get-tuple-element.35), channel_id=1, source_target_pairs={{0,4},{2,6},{4,0},{6,2},{8,12},{10,14},{12,8},{14,10},{16,20},{18,... | collective-permute-start | bytes 1572872 | tf_op jit(solution)/shard_map/ppermute | solution.py:426
  43.0 14.9 %copy-start.12 = (bf16[256,512]{1,0:T(8,128)(2,1)S(1)}, bf16[256,512]{1,0:T(8,128)(2,1)}, u32[]{:S(2)}) copy-start(bf16[256,512]{1,0:T(8,128)(2,1)} %get-tuple-element.38) | copy-start | bytes 786436
  43.1 16.1 %copy-start.10 = (bf16[4,4]{1,0:T(4,128)(2,1)S(1)}, bf16[4,4]{1,0:T(4,128)(2,1)}, u32[]{:S(2)}) copy-start(bf16[4,4]{1,0:T(4,128)(2,1)} %param.15) | copy-start | bytes 100
  56.4 14.1 %copy-start.1 = (bf16[1024,512]{1,0:T(8,128)(2,1)S(1)}, bf16[1024,512]{1,0:T(8,128)(2,1)}, u32[]{:S(2)}) copy-start(bf16[1024,512]{1,0:T(8,128)(2,1)} %refs_11_.1) | copy-start | bytes 3145732
  56.5 7.5 %collective-permute-start.8 = (bf16[256,512]{1,0:T(8,128)(2,1)}, bf16[256,512]{1,0:T(8,128)(2,1)S(1)}, u32[]{:S(2)}, u32[]{:S(2)}) collective-permute-start(bf16[256,512]{1,0:T(8,128)(2,1)} %get-tuple-element.36), channel_id=1, source_target_pairs={{1,0},{0,1},{3,2},{2,3},{5,4},{4,5},{7,6},{6,7},{9,8},{8,9},{11,10... | collective-permute-start | bytes 786440 | tf_op jit(solution)/shard_map/ppermute | solution.py:479
  58.0 12.5 %collective-permute-start.9 = (bf16[256,512]{1,0:T(8,128)(2,1)S(1)}, bf16[256,512]{1,0:T(8,128)(2,1)S(1)}, u32[]{:S(2)}, u32[]{:S(2)}) collective-permute-start(bf16[256,512]{1,0:T(8,128)(2,1)S(1)} %copy-done.12), channel_id=1, source_target_pairs={{1,4},{3,6},{5,0},{7,2},{9,12},{11,14},{13,8},{15,10},{17,20},{19,... | collective-permute-start | bytes 786440 | tf_op jit(solution)/shard_map/ppermute | solution.py:468
  70.5 1.0 %copy-start.11 = (bf16[256,1024]{1,0:T(8,128)(2,1)S(1)}, bf16[256,1024]{1,0:T(8,128)(2,1)}, u32[]{:S(2)}) copy-start(bf16[256,1024]{1,0:T(8,128)(2,1)} %get-tuple-element.34) | copy-start | bytes 1572868
where the time goes:
time: 74.7 us; the launch traced here: 73.3 us
  Pallas kernels  36.1 us (48%)
  waiting for transfers between devices  16.8 us (22%)
  starting transfers between devices  11.3 us (15%)
  local copies, waits for them, and re-layouts  5.18 us (7%)
  matrix products  2.2 us (3%)
  other arithmetic  1.45 us (2%)
    pallas_call x2, Pallas kernels, attend(): pl.pallas_call(body, out_shape=tuple(out_shape), grid_spec=pltpu.Prefetch...  29.1 us
    ppermute x8, starting transfers between devices, move(): return lax.ppermute(block, 'tm', route)  8.62 us
    pallas_call x1, Pallas kernels, project(): pl.pallas_call(body, out_shape=(jax.ShapeDtypeStruct((rows, width), jnp.b...  7.01 us
    ppermute x8, waiting for transfers between devices, move(): return lax.ppermute(block, 'tm', route)  6.81 us
    ppermute x1, waiting for transfers between devices, on_device(): other_branches.append(lax.ppermute(away_branch, ('tm', 'series'), route))  6.43 us
    ppermute x1, waiting for transfers between devices, on_device(): mine_branches.append(lax.ppermute(mine_branch, 'series', route))  3.6 us
    unnamed x26, local copies, waits for them, and re-layouts  2.78 us
    squeeze x1, local copies, waits for them, and re-layouts, part(): return lax.dynamic_index_in_dim(array, index, 0, keepdims=False)  2.18 us
  transfers between devices with their start and end apart: 10, of which 4 were waited for; matrix products, arithmetic and copies ran while one was open for 2% of the time, Pallas kernels for 49%

commit v1 on v0

--- a/solution.py
+++ b/solution.py
@@ -107,7 +107,7 @@
         take = lambda count: [refs.pop(0) for _ in range(count)]
         raw_refs = take(raw_count)
         ready_refs = take(2 * ready_count)
-        rows_ref, query_ref = take(2) if home else (raw_refs[0], None)
+        rows_hbm, query_ref = take(2) if home else (None, None)
         wq_ref = None if home else take(1)[0]
         wk_ref, wv_ref, wo_hbm, down_hbm = take(4)
         hidden_ref, branch_ref = take(2)
@@ -115,6 +115,7 @@
         key_scr, row_scr, query_scr = take(3)
         value_scrs, score_scrs, top_scrs = take(2), take(2), take(2)
         attended_scr, update_scr, wo_scr, down_scr, copy_sems = take(5)
+        rows_ref = take(1)[0] if home else raw_refs[0]
         index = pl.program_id(0)
         position = place_ref[0]
         core = position % 2
@@ -132,6 +133,8 @@
             pltpu.make_async_copy(wo_hbm, wo_scr, copy_sems.at[0]),
             pltpu.make_async_copy(down_hbm, down_scr, copy_sems.at[1]),
         ]
+        if home:
+            copies.append(pltpu.make_async_copy(rows_hbm, rows_ref, copy_sems.at[2]))
 
         @pl.when(index == 0)
         def _():
@@ -218,12 +221,13 @@
                 )
                 key_row = row_scr[start:stop, :]
                 key_row = jnp.concatenate([key_row] * (cols // LANES), 1)
-                allowed = None
-                if step <= reach:
+                if step < reach:
                     allowed = key_row >= lowest - first
-                if step >= reach:
-                    upper = key_row <= highest - first
-                    allowed = upper if allowed is None else allowed & upper
+                elif step > reach:
+                    allowed = key_row <= highest - first
+                else:
+                    above = (key_row - (lowest - first)).astype(jnp.uint32)
+                    allowed = above <= (highest - lowest).astype(jnp.uint32)
                 scores = jnp.where(allowed, scores, MASKED)
                 score_scr[pair, half, step, start:stop, :] = scores
                 top = jnp.max(scores, axis=0, keepdims=True)
@@ -358,7 +362,7 @@
         operands += [keys, values]
     whole = lambda shape: pl.BlockSpec(shape, lambda g, *_: (0, 0))
     if home:
-        in_specs += [whole((rows, width)), block]
+        in_specs += [pl.BlockSpec(memory_space=pl.ANY), block]
         operands += own
     else:
         in_specs.append(weight_spec(0))
@@ -399,8 +403,9 @@
                 pltpu.VMEM((rows, width), jnp.float32),
                 pltpu.VMEM(output_proj.shape, jnp.bfloat16),
                 pltpu.VMEM(mixer_down.shape, jnp.bfloat16),
-                pltpu.SemaphoreType.DMA((2,)),
-            ],
+                pltpu.SemaphoreType.DMA((3,)),
+            ]
+            + [pltpu.VMEM((rows, width), jnp.bfloat16)] * home,
         ),
         cost_estimate=pl.CostEstimate(
             flops=(8 * steps * rows + 4 * raw_count * width) * rows * width,

time: 74.7 us -> 74.2 us (level)
  no operation moved by 1% of the time
where the time goes in v1:
time: 74.2 us; the launch traced here: 72.9 us
  Pallas kernels  35.7 us (48%)
  waiting for transfers between devices  16.9 us (23%)
  starting transfers between devices  11.3 us (15%)
  local copies, waits for them, and re-layouts  5.18 us (7%)
  matrix products  2.19 us (3%)
  other arithmetic  1.45 us (2%)
    pallas_call x2, Pallas kernels, attend(): pl.pallas_call(body, out_shape=tuple(out_shape), grid_spec=pltpu.Prefetch...  28.7 us
    ppermute x8, starting transfers between devices, move(): return lax.ppermute(block, 'tm', route)  8.62 us
    pallas_call x1, Pallas kernels, project(): pl.pallas_call(body, out_shape=(jax.ShapeDtypeStruct((rows, width), jnp.b...  7.01 us
    ppermute x8, waiting for transfers between devices, move(): return lax.ppermute(block, 'tm', route)  6.81 us
    ppermute x1, waiting for transfers between devices, on_device(): other_branches.append(lax.ppermute(away_branch, ('tm', 'series'), route))  6.44 us
    ppermute x1, waiting for transfers between devices, on_device(): mine_branches.append(lax.ppermute(mine_branch, 'series', route))  3.61 us
    unnamed x26, local copies, waits for them, and re-layouts  2.78 us
    squeeze x1, local copies, waits for them, and re-layouts, part(): return lax.dynamic_index_in_dim(array, index, 0, keepdims=False)  2.18 us
  transfers between devices with their start and end apart: 10, of which 4 were waited for; matrix products, arithmetic and copies ran while one was open for 2% of the time, Pallas kernels for 49%

profile of v1, /device:TPU:0, one launch (start us, length us, event | category | flops | bytes accessed | tf_op | source)
XLA Modules:
  0.0 72.9 jit_solution(3657125242440329612)
XLA Ops:
  0.0 2.2 %dynamic-slice_bitcast_fusion = (bf16[256,1024]{1,0:T(8,128)(2,1)S(1)}, bf16[256,1024]{1,0:T(8,128)(2,1)}) fusion(bf16[2,256,1024]{2,1,0:T(8,128)(2,1)} %param.8, s32[]{:T(128)S(6)} %select_n.67, s32[]{:T(128)S(6)} %select_n.66), kind=kLoop, calls=%fused_computation.6 | loop fusion | bytes 2097160 | tf_op jit(solution)/shard_map/jit(dynamic_index_in_dim)/squeeze | solution.py:434
  2.2 0.5 collective-permute-start.1
  2.7 2.5 %collective-permute-start = (bf16[256,1024]{1,0:T(8,128)(2,1)}, bf16[256,1024]{1,0:T(8,128)(2,1)S(1)}, u32[]{:S(2)}, u32[]{:S(2)}) collective-permute-start(bf16[256,1024]{1,0:T(8,128)(2,1)} %get-tuple-element.44), channel_id=1, source_target_pairs={{0,4},{2,6},{4,0},{6,2},{8,12},{10,14},{12,8},{14,10},{16,20},{18,... | collective-permute-start | bytes 1572872 | tf_op jit(solution)/shard_map/ppermute | solution.py:431
  5.2 1.3 %collective-permute-start.2 = (bf16[256,1024]{1,0:T(8,128)(2,1)S(1)}, bf16[256,1024]{1,0:T(8,128)(2,1)S(1)}, u32[]{:S(2)}, u32[]{:S(2)}) collective-permute-start(bf16[256,1024]{1,0:T(8,128)(2,1)S(1)} %get-tuple-element.43.first_ref.refs_6_), channel_id=1, source_target_pairs={{4,12},{6,14},{8,0},{10,2},{12,20},{14,22},{16,8},{18,10},{20,28},... | collective-permute-start | bytes 1572872 | tf_op jit(solution)/shard_map/ppermute | solution.py:431
  6.5 0.0 collective-permute-done.1.beside_ref
  6.5 0.8 %copy-done.9 = bf16[256,1024]{1,0:T(8,128)(2,1)} copy-done((bf16[256,1024]{1,0:T(8,128)(2,1)}, bf16[256,1024]{1,0:T(8,128)(2,1)S(1)}, u32[]{:S(2)}) %copy-start.9) | copy-done | bytes 524312
  7.3 7.0 %project.1 = (bf16[256,1024]{1,0:T(8,128)(2,1)}, bf16[2,256,1024]{2,1,0:T(8,128)(2,1)}, bf16[2,1024,256]{2,1,0:T(8,128)(2,1)}) custom-call(bf16[256,1024]{1,0:T(8,128)(2,1)} %copy-done.2, bf16[256,1024]{1,0:T(8,128)(2,1)} %copy-done.9, bf16[1024,3072]{1,0:T(8,128)(2,1)} %refs_9_.3, bf16[1024,3072]{1,0:T(8,128)(2,1)} %refs_9_.3, bf16[1024,3072]{1,0:T(8,128)(2,1)} %refs_9_.3), custom_call_target="tpu_custom_call" | custom-call | flops 2684354560 | bytes 6291456 | tf_op jit(solution)/shard_map/project/pallas_call | solution.py:56
  14.3 3.7 %collective-permute-done.refs_0_ = bf16[256,1024]{1,0:T(8,128)(2,1)S(1)} collective-permute-done((bf16[256,1024]{1,0:T(8,128)(2,1)}, bf16[256,1024]{1,0:T(8,128)(2,1)S(1)}, u32[]{:S(2)}, u32[]{:S(2)}) %collective-permute-start) | collective-permute-done | bytes 524320 | tf_op jit(solution)/shard_map/ppermute | solution.py:431
  18.0 0.0 collective-permute-start.3
  18.0 3.1 %collective-permute-done.2.refs_2_ = bf16[256,1024]{1,0:T(8,128)(2,1)S(1)} collective-permute-done((bf16[256,1024]{1,0:T(8,128)(2,1)S(1)}, bf16[256,1024]{1,0:T(8,128)(2,1)S(1)}, u32[]{:S(2)}, u32[]{:S(2)}) %collective-permute-start.2) | collective-permute-done | bytes 524320 | tf_op jit(solution)/shard_map/ppermute | solution.py:431
  21.1 0.1 collective-permute-start.4
  21.2 3.5 %collective-permute-start.5 = (bf16[256,1024]{1,0:T(8,128)(2,1)S(1)}, bf16[256,1024]{1,0:T(8,128)(2,1)S(1)}, u32[]{:S(2)}, u32[]{:S(2)}) collective-permute-start(bf16[256,1024]{1,0:T(8,128)(2,1)S(1)} %collective-permute-done.refs_0_), channel_id=1, source_target_pairs={{0,8},{2,10},{8,16},{10,18},{12,4},{14,6},{16,24},{18,26},{20,12},... | collective-permute-start | bytes 1572872 | tf_op jit(solution)/shard_map/ppermute | solution.py:431
  24.7 0.7 collective-permute-start.6
  25.4 0.0 collective-permute-done.4.refs_3_
  25.5 0.8 %copy-done.8 = bf16[256,1024]{1,0:T(8,128)(2,1)} copy-done((bf16[256,1024]{1,0:T(8,128)(2,1)}, bf16[256,1024]{1,0:T(8,128)(2,1)S(1)}, u32[]{:S(2)}) %copy-start.8) | copy-done | bytes 524312
  26.3 15.5 %attend.2 = (bf16[256,1024]{1,0:T(8,128)(2,1)}, bf16[256,512]{1,0:T(8,128)(2,1)}, bf16[2,256,1024]{2,1,0:T(8,128)(2,1)}, bf16[2,1024,256]{2,1,0:T(8,128)(2,1)}) custom-call(s32[1]{0:T(128)} %bitcast.place_ref, s32[16]{0:T(128)} %window_ref.3, s32[2]{0:T(128)} %length_ref.3, bf16[256,1024]{1,0:T(8,128)(2,1)} %copy-done.3, bf16[256,1024]{1,0:T(8,128)(2,1)} %copy-done.7, ...), custom_call_target="tpu_custom_call" | custom-call | flops 6979321856 | bytes 9437184 | tf_op jit(solution)/shard_map/attend/pallas_call | solution.py:385
  41.8 0.0 collective-permute-done.6.refs_1_
  41.8 0.1 collective-permute-start.7
  41.9 0.7 copy-done.5
  42.6 0.2 copy-done.6
  42.8 13.1 %attend.3 = (bf16[256,1024]{1,0:T(8,128)(2,1)}, bf16[256,512]{1,0:T(8,128)(2,1)}) custom-call(s32[1]{0:T(128)} %bitcast.place_ref, s32[16]{0:T(128)} %window_ref.3, s32[2]{0:T(128)} %length_ref.3, bf16[256,1024]{1,0:T(8,128)(2,1)} %copy-done.5, bf16[256,1024]{1,0:T(8,128)(2,1)} %copy-done.6, bf16[2,256,1024]{2,1,0:T(8,128)(2,1)} %get-tuple-element.26.refs_4_.refs_2_, ...), custom_call_target="tpu_custom_call" | custom-call | flops 4831838208 | bytes 9437184 | tf_op jit(solution)/shard_map/attend/pallas_call | solution.py:385
  56.0 0.0 copy-start.1
  56.0 1.6 %collective-permute-start.8 = (bf16[256,512]{1,0:T(8,128)(2,1)}, bf16[256,512]{1,0:T(8,128)(2,1)S(1)}, u32[]{:S(2)}, u32[]{:S(2)}) collective-permute-start(bf16[256,512]{1,0:T(8,128)(2,1)} %get-tuple-element.36), channel_id=1, source_target_pairs={{1,0},{0,1},{3,2},{2,3},{5,4},{4,5},{7,6},{6,7},{9,8},{8,9},{11,10... | collective-permute-start | bytes 786440 | tf_op jit(solution)/shard_map/ppermute | solution.py:484
  57.5 1.1 %collective-permute-start.9 = (bf16[256,512]{1,0:T(8,128)(2,1)S(1)}, bf16[256,512]{1,0:T(8,128)(2,1)S(1)}, u32[]{:S(2)}, u32[]{:S(2)}) collective-permute-start(bf16[256,512]{1,0:T(8,128)(2,1)S(1)} %copy-done.12), channel_id=1, source_target_pairs={{1,4},{3,6},{5,0},{7,2},{9,12},{11,14},{13,8},{15,10},{17,20},{19,... | collective-permute-start | bytes 786440 | tf_op jit(solution)/shard_map/ppermute | solution.py:473
  58.7 0.2 dynamic-slice_reduce_fusion.3
  58.9 1.0 %convert_element_type.29 = f32[256,512]{1,0:T(8,128)S(1)} convert(bf16[256,512]{1,0:T(8,128)(2,1)} %get-tuple-element.36) | non-fusion elementwise | flops 131072 | bytes 786432 | tf_op jit(solution)/shard_map/convert_element_type | solution.py:500
  59.9 3.6 %collective-permute-done.8 = bf16[256,512]{1,0:T(8,128)(2,1)S(1)} collective-permute-done((bf16[256,512]{1,0:T(8,128)(2,1)}, bf16[256,512]{1,0:T(8,128)(2,1)S(1)}, u32[]{:S(2)}, u32[]{:S(2)}) %collective-permute-start.8) | collective-permute-done | bytes 262176 | tf_op jit(solution)/shard_map/ppermute | solution.py:484
  63.6 6.4 %collective-permute-done.9 = bf16[256,512]{1,0:T(8,128)(2,1)S(1)} collective-permute-done((bf16[256,512]{1,0:T(8,128)(2,1)S(1)}, bf16[256,512]{1,0:T(8,128)(2,1)S(1)}, u32[]{:S(2)}, u32[]{:S(2)}) %collective-permute-start.9) | collective-permute-done | bytes 262176 | tf_op jit(solution)/shard_map/ppermute | solution.py:473
  70.1 0.4 fusion
  70.5 0.3 add_convert_fusion.1
  70.9 0.2 copy-done.11
  71.1 1.8 %add_convert_fusion = bf16[2,256,1024]{2,1,0:T(8,128)(2,1)} fusion(bf16[2,256,512]{2,1,0:T(8,128)(2,1)S(1)} %add_convert_fusion.1, bf16[1,256,1024]{2,1,0:T(8,128)(2,1)S(1)} %bitcast.13, bf16[1,256,1024]{2,1,0:T(8,128)(2,1)S(1)} %bitcast.14, bf16[512,1024]{1,0:T(8,128)(2,1)S(1)} %copy-done, pred[]{:T(512)S(6)} %eq.9), kind=kOutput, calls=%fused_computation | convolution fusion | flops 540016640 | bytes 3670017 | tf_op jit(solution)/shard_map/spc,cd->spd/dot_general | solution.py:502
  (26 shorter events, 0.1 us)
Async XLA Ops:
  0.0 70.9 %copy-start = (bf16[512,1024]{1,0:T(8,128)(2,1)S(1)}, bf16[512,1024]{1,0:T(8,128)(2,1)}, u32[]{:S(2)}) copy-start(bf16[512,1024]{1,0:T(8,128)(2,1)} %param.14) | copy-start | bytes 3145732
  2.2 4.3 %copy-start.2 = (bf16[256,1024]{1,0:T(8,128)(2,1)}, bf16[256,1024]{1,0:T(8,128)(2,1)S(1)}, u32[]{:S(2)}) copy-start(bf16[256,1024]{1,0:T(8,128)(2,1)S(1)} %get-tuple-element.43.first_ref.refs_6_) | copy-start | bytes 1572868
  2.2 4.3 %collective-permute-start.1 = (bf16[256,1024]{1,0:T(8,128)(2,1)S(1)}, bf16[256,1024]{1,0:T(8,128)(2,1)S(1)}, u32[]{:S(2)}, u32[]{:S(2)}) collective-permute-start(bf16[256,1024]{1,0:T(8,128)(2,1)S(1)} %get-tuple-element.43.first_ref.refs_6_), channel_id=1, source_target_pairs={{0,2},{2,0},{4,6},{6,4},{8,10},{10,8},{12,14},{14,12},{16,18},{18,... | collective-permute-start | bytes 1572872 | tf_op jit(solution)/shard_map/ppermute | solution.py:431
  2.7 15.3 %collective-permute-start = (bf16[256,1024]{1,0:T(8,128)(2,1)}, bf16[256,1024]{1,0:T(8,128)(2,1)S(1)}, u32[]{:S(2)}, u32[]{:S(2)}) collective-permute-start(bf16[256,1024]{1,0:T(8,128)(2,1)} %get-tuple-element.44), channel_id=1, source_target_pairs={{0,4},{2,6},{4,0},{6,2},{8,12},{10,14},{12,8},{14,10},{16,20},{18,... | collective-permute-start | bytes 1572872 | tf_op jit(solution)/shard_map/ppermute | solution.py:431
  5.2 15.9 %collective-permute-start.2 = (bf16[256,1024]{1,0:T(8,128)(2,1)S(1)}, bf16[256,1024]{1,0:T(8,128)(2,1)S(1)}, u32[]{:S(2)}, u32[]{:S(2)}) collective-permute-start(bf16[256,1024]{1,0:T(8,128)(2,1)S(1)} %get-tuple-element.43.first_ref.refs_6_), channel_id=1, source_target_pairs={{4,12},{6,14},{8,0},{10,2},{12,20},{14,22},{16,8},{18,10},{20,28},... | collective-permute-start | bytes 1572872 | tf_op jit(solution)/shard_map/ppermute | solution.py:431
  6.5 0.8 %copy-start.9 = (bf16[256,1024]{1,0:T(8,128)(2,1)}, bf16[256,1024]{1,0:T(8,128)(2,1)S(1)}, u32[]{:S(2)}) copy-start(bf16[256,1024]{1,0:T(8,128)(2,1)S(1)} %collective-permute-done.1.beside_ref) | copy-start | bytes 1572868
  18.0 8.3 %copy-start.3 = (bf16[256,1024]{1,0:T(8,128)(2,1)}, bf16[256,1024]{1,0:T(8,128)(2,1)S(1)}, u32[]{:S(2)}) copy-start(bf16[256,1024]{1,0:T(8,128)(2,1)S(1)} %collective-permute-done.refs_0_) | copy-start | bytes 1572868
  18.0 3.1 %collective-permute-start.3 = (bf16[256,1024]{1,0:T(8,128)(2,1)S(1)}, bf16[256,1024]{1,0:T(8,128)(2,1)S(1)}, u32[]{:S(2)}, u32[]{:S(2)}) collective-permute-start(bf16[256,1024]{1,0:T(8,128)(2,1)S(1)} %collective-permute-done.refs_0_), channel_id=1, source_target_pairs={{0,2},{2,0},{4,6},{6,4},{8,10},{10,8},{12,14},{14,12},{16,18},{18,... | collective-permute-start | bytes 1572872 | tf_op jit(solution)/shard_map/ppermute | solution.py:431
  21.1 5.1 %copy-start.4 = (bf16[256,1024]{1,0:T(8,128)(2,1)}, bf16[256,1024]{1,0:T(8,128)(2,1)S(1)}, u32[]{:S(2)}) copy-start(bf16[256,1024]{1,0:T(8,128)(2,1)S(1)} %collective-permute-done.2.refs_2_) | copy-start | bytes 1572868
  21.1 4.3 %copy-start.7 = (bf16[256,1024]{1,0:T(8,128)(2,1)}, bf16[256,1024]{1,0:T(8,128)(2,1)S(1)}, u32[]{:S(2)}) copy-start(bf16[256,1024]{1,0:T(8,128)(2,1)S(1)} %collective-permute-done.3.refs_1_) | copy-start | bytes 1572868
  21.1 4.3 %collective-permute-start.4 = (bf16[256,1024]{1,0:T(8,128)(2,1)S(1)}, bf16[256,1024]{1,0:T(8,128)(2,1)S(1)}, u32[]{:S(2)}, u32[]{:S(2)}) collective-permute-start(bf16[256,1024]{1,0:T(8,128)(2,1)S(1)} %collective-permute-done.2.refs_2_), channel_id=1, source_target_pairs={{0,2},{2,0},{4,6},{6,4},{8,10},{10,8},{12,14},{14,12},{16,18},{18,... | collective-permute-start | bytes 1572872 | tf_op jit(solution)/shard_map/ppermute | solution.py:431
  21.2 20.6 %collective-permute-start.5 = (bf16[256,1024]{1,0:T(8,128)(2,1)S(1)}, bf16[256,1024]{1,0:T(8,128)(2,1)S(1)}, u32[]{:S(2)}, u32[]{:S(2)}) collective-permute-start(bf16[256,1024]{1,0:T(8,128)(2,1)S(1)} %collective-permute-done.refs_0_), channel_id=1, source_target_pairs={{0,8},{2,10},{8,16},{10,18},{12,4},{14,6},{16,24},{18,26},{20,12},... | collective-permute-start | bytes 1572872 | tf_op jit(solution)/shard_map/ppermute | solution.py:431
  24.7 17.1 %collective-permute-start.6 = (bf16[256,1024]{1,0:T(8,128)(2,1)S(1)}, bf16[256,1024]{1,0:T(8,128)(2,1)S(1)}, u32[]{:S(2)}, u32[]{:S(2)}) collective-permute-start(bf16[256,1024]{1,0:T(8,128)(2,1)S(1)} %collective-permute-done.refs_0_), channel_id=1, source_target_pairs={{2,8},{10,16},{12,6},{18,24},{20,14},{28,22},{3,9},{11,17},{13,7},... | collective-permute-start | bytes 1572872 | tf_op jit(solution)/shard_map/ppermute | solution.py:431
  25.4 0.8 %copy-start.8 = (bf16[256,1024]{1,0:T(8,128)(2,1)}, bf16[256,1024]{1,0:T(8,128)(2,1)S(1)}, u32[]{:S(2)}) copy-start(bf16[256,1024]{1,0:T(8,128)(2,1)S(1)} %collective-permute-done.4.refs_3_) | copy-start | bytes 1572868
  41.8 0.8 %copy-start.5 = (bf16[256,1024]{1,0:T(8,128)(2,1)}, bf16[256,1024]{1,0:T(8,128)(2,1)S(1)}, u32[]{:S(2)}) copy-start(bf16[256,1024]{1,0:T(8,128)(2,1)S(1)} %collective-permute-done.5.refs_0_) | copy-start | bytes 1572868
  41.8 1.0 %copy-start.6 = (bf16[256,1024]{1,0:T(8,128)(2,1)}, bf16[256,1024]{1,0:T(8,128)(2,1)S(1)}, u32[]{:S(2)}) copy-start(bf16[256,1024]{1,0:T(8,128)(2,1)S(1)} %collective-permute-done.6.refs_1_) | copy-start | bytes 1572868
  41.8 28.2 %collective-permute-start.7 = (bf16[256,1024]{1,0:T(8,128)(2,1)}, bf16[256,1024]{1,0:T(8,128)(2,1)S(1)}, u32[]{:S(2)}, u32[]{:S(2)}) collective-permute-start(bf16[256,1024]{1,0:T(8,128)(2,1)} %get-tuple-element.35), channel_id=1, source_target_pairs={{0,4},{2,6},{4,0},{6,2},{8,12},{10,14},{12,8},{14,10},{16,20},{18,... | collective-permute-start | bytes 1572872 | tf_op jit(solution)/shard_map/ppermute | solution.py:431
  42.8 14.7 %copy-start.12 = (bf16[256,512]{1,0:T(8,128)(2,1)S(1)}, bf16[256,512]{1,0:T(8,128)(2,1)}, u32[]{:S(2)}) copy-start(bf16[256,512]{1,0:T(8,128)(2,1)} %get-tuple-element.38) | copy-start | bytes 786436
  42.8 15.8 %copy-start.10 = (bf16[4,4]{1,0:T(4,128)(2,1)S(1)}, bf16[4,4]{1,0:T(4,128)(2,1)}, u32[]{:S(2)}) copy-start(bf16[4,4]{1,0:T(4,128)(2,1)} %param.15) | copy-start | bytes 100
  56.0 14.1 %copy-start.1 = (bf16[1024,512]{1,0:T(8,128)(2,1)S(1)}, bf16[1024,512]{1,0:T(8,128)(2,1)}, u32[]{:S(2)}) copy-start(bf16[1024,512]{1,0:T(8,128)(2,1)} %refs_11_.1) | copy-start | bytes 3145732
  56.0 7.5 %collective-permute-start.8 = (bf16[256,512]{1,0:T(8,128)(2,1)}, bf16[256,512]{1,0:T(8,128)(2,1)S(1)}, u32[]{:S(2)}, u32[]{:S(2)}) collective-permute-start(bf16[256,512]{1,0:T(8,128)(2,1)} %get-tuple-element.36), channel_id=1, source_target_pairs={{1,0},{0,1},{3,2},{2,3},{5,4},{4,5},{7,6},{6,7},{9,8},{8,9},{11,10... | collective-permute-start | bytes 786440 | tf_op jit(solution)/shard_map/ppermute | solution.py:484
  57.5 12.5 %collective-permute-start.9 = (bf16[256,512]{1,0:T(8,128)(2,1)S(1)}, bf16[256,512]{1,0:T(8,128)(2,1)S(1)}, u32[]{:S(2)}, u32[]{:S(2)}) collective-permute-start(bf16[256,512]{1,0:T(8,128)(2,1)S(1)} %copy-done.12), channel_id=1, source_target_pairs={{1,4},{3,6},{5,0},{7,2},{9,12},{11,14},{13,8},{15,10},{17,20},{19,... | collective-permute-start | bytes 786440 | tf_op jit(solution)/shard_map/ppermute | solution.py:473
  70.1 1.0 %copy-start.11 = (bf16[256,1024]{1,0:T(8,128)(2,1)S(1)}, bf16[256,1024]{1,0:T(8,128)(2,1)}, u32[]{:S(2)}) copy-start(bf16[256,1024]{1,0:T(8,128)(2,1)} %get-tuple-element.34) | copy-start | bytes 1572868
